TPU v7x, 256 devices: a whole 4x4x8 slice. The times are simulated.
256 devices in a mesh: tile: 64 (over y, z, x_hi), band: 4 (over x_lo, core).
Axes of the slice: x: 4 (x_hi: 2, x_lo: 2; x = x_hi * 2 + x_lo), y: 4, z: 8, core: 2. Of those that a mesh axis runs over, the one named last changes fastest.
Arguments:
- background: float32 [36, 36, 64, 8, 128], P('band', None, 'tile'), may hold values from 0.2 to 2
- tangent: float32 [36, 36, 64, 8, 128], P('band', None, 'tile'), may hold values from -6 to 6
- sea_mask: int32 [64, 8, 128], P('tile'), may hold values 0 or 1
- coupling: float32 [36], P('band'), may hold values from 0.005 to 0.05
- freq_offsets: int32 [2], replicated, may hold values from 1 to 3, as said below
- dir_offsets: int32 [2], replicated, may hold values from 1 to 5
Outputs:
- background_out: float32 [36, 36, 64, 8, 128], P('band', None, 'tile')
- tangent_out: float32 [36, 36, 64, 8, 128], P('band', None, 'tile')
Inputs may be any that keep to these rules, and one draw needn't show every extreme that they name: `freq_offsets`: one of the two offsets equals 3, the other is smaller.
All inputs are finite; a program needn't handle non-finite values. No bound on the sum of `sea_mask` on one device may be relied on, other than what follows from the above.
Results may differ from a plain program's by a relative error of at most 0.00002.
Values sent between devices are 32-bit elements; how exact they have to be, the bound alone decides.
A program may use at most 64 MiB of HBM per device.

v0:
```python
import math

import jax
import jax.numpy as jnp
from jax import lax
from jax.experimental import pallas as pl
from jax.experimental.pallas import tpu as pltpu
from jax.sharding import PartitionSpec as P

TY = 4
FH = 3
STEPS = 2
ND = 36
PAD = 5
WIDE = ND + 2 * PAD
HALF = ND // 2
GROUP = 3
MESH = pl.DeviceIdType.MESH

weight_plus = 1.0 / 1.25**4
weight_minus = 1.0 / 0.75**4
weight_cross = 1.0 / (1.0 - 0.25**2) ** 4
source_step = 0.5

COS = [math.cos((j + 0.5) * 2.0 * math.pi / ND) for j in range(ND)]
SIN = [math.sin((j + 0.5) * 2.0 * math.pi / ND) for j in range(ND)]
EASTWARD = [j for j in range(ND) if COS[j] > 0]
WESTWARD = [j for j in range(ND) if COS[j] < 0]
NORTHWARD = [j for j in range(ND) if SIN[j] > 0]
SOUTHWARD = [j for j in range(ND) if SIN[j] < 0]


def kernel(
    n_k,
    back_in,
    tang_in,
    mask_in,
    coupling,
    freq_off,
    dir_off,
    back_out,
    tang_out,
    state,
    low_ext_0,
    low_ext_1,
    high_ext_0,
    high_ext_1,
    row_send,
    row_recv,
    col_send,
    col_recv,
    speed,
    row_ssem,
    row_rsem,
    col_ssem,
    col_rsem,
    band_ssem,
    band_rsem,
):
    tiles = lax.axis_size("tile")
    bands = lax.axis_size("band")
    tile = lax.axis_index("tile")
    band = lax.axis_index("band")
    lat = lax.rem(tile + TY // 2, TY)
    north = lax.rem(tile + 1, tiles)
    south = lax.rem(tile + tiles - 1, tiles)
    east = lax.rem(tile + TY, tiles)
    west = lax.rem(tile + tiles - TY, tiles)
    has_north = lat < TY - 1
    has_south = lat > 0
    has_up = band < bands - 1
    has_down = band > 0
    groups = n_k // GROUP
    low_exts = (low_ext_0, low_ext_1)
    high_exts = (high_ext_0, high_ext_1)
    inputs = (back_in, tang_in)
    outputs = (back_out, tang_out)

    def row_copy(slot, side, g):
        ks = pl.ds(g * GROUP, GROUP)
        return pltpu.make_async_remote_copy(
            src_ref=row_send.at[slot, side, ks],
            dst_ref=row_recv.at[slot, side, ks],
            send_sem=row_ssem.at[slot, side, g],
            recv_sem=row_rsem.at[slot, side, g],
            device_id={"tile": north if side == 0 else south},
            device_id_type=MESH,
        )

    def col_copy(slot, side, g):
        return pltpu.make_async_remote_copy(
            src_ref=col_send.at[slot, side, g],
            dst_ref=col_recv.at[slot, side, g],
            send_sem=col_ssem.at[slot, side, g],
            recv_sem=col_rsem.at[slot, side, g],
            device_id={"tile": east if side == 0 else west},
            device_id_type=MESH,
        )

    def band_copy(step, side):
        if side == 0:
            src = state.at[step, :, pl.ds(n_k - FH, FH), pl.ds(PAD, ND)]
            dst = low_exts[step].at[:, pl.ds(0, FH), pl.ds(PAD, ND)]
            target = lax.rem(band + 1, bands)
        else:
            src = state.at[step, :, pl.ds(0, FH), pl.ds(PAD, ND)]
            dst = high_exts[step].at[:, pl.ds(FH - 1, FH), pl.ds(PAD, ND)]
            target = lax.rem(band + bands - 1, bands)
        return pltpu.make_async_remote_copy(
            src_ref=src,
            dst_ref=dst,
            send_sem=band_ssem.at[step, side],
            recv_sem=band_rsem.at[step, side],
            device_id={"band": target},
            device_id_type=MESH,
        )

    def send_halo(slot, g):
        @pl.when(has_north)
        def _():
            row_copy(slot, 0, g).start()

        @pl.when(has_south)
        def _():
            row_copy(slot, 1, g).start()

        col_copy(slot, 0, g).start()
        col_copy(slot, 1, g).start()

    def wait_halo(slot, g):
        @pl.when(has_south)
        def _():
            row_copy(slot, 0, g).wait_recv()

        @pl.when(has_north)
        def _():
            row_copy(slot, 1, g).wait_recv()

        col_copy(slot, 0, g).wait_recv()
        col_copy(slot, 1, g).wait_recv()

    barrier = pltpu.get_barrier_semaphore()
    for cond, target in (
        (None, {"tile": east}),
        (None, {"tile": west}),
        (has_north, {"tile": north}),
        (has_south, {"tile": south}),
        (has_up, {"band": lax.rem(band + 1, bands)}),
        (has_down, {"band": lax.rem(band + bands - 1, bands)}),
    ):

        def greet(target=target):
            pl.semaphore_signal(barrier, inc=1, device_id=target, device_id_type=MESH)

        if cond is None:
            greet()
        else:
            pl.when(cond)(greet)

    base = jnp.float32(0.7)
    for b in range(1, 4):
        base = jnp.where(band == b, jnp.float32(0.7 * 1.1 ** (-n_k * b)), base)
    for k in range(n_k):
        speed[k] = base * jnp.float32(1.1 ** (-k))

    lane = lax.broadcasted_iota(jnp.int32, (8, 128), 1)
    sub = lax.broadcasted_iota(jnp.int32, (8, 128), 0)
    mask = mask_in[0].astype(jnp.float32)
    zeros = jnp.zeros((8, 128), jnp.float32)

    def zero_rows(side):
        def slots(i, _):
            row_recv[i // n_k, side, lax.rem(i, n_k)] = jnp.zeros((ND, 128), jnp.float32)
            return 0

        lax.fori_loop(0, 2 * STEPS * n_k, slots, 0)

    pl.when(jnp.logical_not(has_south))(lambda: zero_rows(0))
    pl.when(jnp.logical_not(has_north))(lambda: zero_rows(1))

    def zero_ext(ext, first):
        def rows(r, _):
            ext[r // FH, first + lax.rem(r, FH)] = jnp.zeros((WIDE, 8, 128), jnp.float32)
            return 0

        lax.fori_loop(0, 2 * FH, rows, 0)

    for step in range(STEPS):
        pl.when(jnp.logical_not(has_down))(lambda: zero_ext(low_exts[step], 0))
        pl.when(jnp.logical_not(has_up))(lambda: zero_ext(high_exts[step], FH - 1))

    def pack_bin(slot, f, k, j, new, parts):
        r = f * HALF + (j if SIN[j] > 0 else j - HALF)
        if SIN[j] > 0:
            row_send[slot, 0, k, pl.ds(r, 1), :] = new[7:8, :]
        else:
            row_send[slot, 1, k, pl.ds(r, 1), :] = new[0:1, :]
        if COS[j] > 0:
            c = f * HALF + EASTWARD.index(j)
            moved = pltpu.roll(new, (c + 1) % 128, 1)
            return [jnp.where(lane == c, moved, parts[0]), parts[1]]
        c = f * HALF + WESTWARD.index(j)
        moved = new if c == 0 else pltpu.roll(new, c, 1)
        return [parts[0], jnp.where(lane == c, moved, parts[1])]

    def join(sums, parts, i):
        return tuple(s + pltpu.roll(p, i * ND, 1) for s, p in zip(sums, parts))

    def finish_pack(slot, g, sums):
        col_send[slot, 0, g] = sums[0]
        col_send[slot, 1, g] = sums[1]

    def write_state(step, f, k, j, new):
        state[step, f, k, PAD + j] = new
        if j >= ND - PAD:
            state[step, f, k, j - (ND - PAD)] = new
        if j < PAD:
            state[step, f, k, PAD + ND + j] = new

    def entry(i, _):
        g = lax.rem(2 * i, groups)

        def at_level(kk, sums):
            k = g * GROUP + kk
            parts = [zeros, zeros]
            for f in range(2):
                for j in range(ND):
                    new = inputs[f][k, j, 0] * mask
                    state[0, f, k, PAD + j] = new
                    parts = pack_bin(0, f, k, j, new, parts)
            return join(sums, parts, kk)

        finish_pack(0, g, lax.fori_loop(0, GROUP, at_level, (zeros, zeros)))
        return 0

    lax.fori_loop(0, groups, entry, 0)

    peers = (
        2
        + has_north.astype(jnp.int32)
        + has_south.astype(jnp.int32)
        + has_up.astype(jnp.int32)
        + has_down.astype(jnp.int32)
    )
    pl.semaphore_wait(barrier, peers)

    for g in (0, 2, 1):
        send_halo(0, g)

    def substep(step, part):
        slot = 2 * step + part

        def group(i, _):
            g = lax.rem(2 * i + step, groups)
            wait_halo(slot, g)
            col_low = col_recv[slot, 0, g]
            col_high = col_recv[slot, 1, g]

            def at_level(kk, sums):
                k = g * GROUP + kk
                rate = speed[k]
                back = lax.rem(128 - kk * ND, 128)
                halo_w = pltpu.roll(col_low, back, 1)
                halo_e = pltpu.roll(col_high, back, 1)
                parts = [zeros, zeros]
                for j in range(ND):
                    rate_x = rate * jnp.float32(abs(COS[j]))
                    rate_y = rate * jnp.float32(abs(SIN[j]))
                    rate_0 = jnp.float32(1.0) - rate_x - rate_y
                    for f in range(2):
                        old = state[step, f, k, PAD + j]
                        if COS[j] > 0:
                            c = f * HALF + EASTWARD.index(j)
                            edge = halo_w if c == 0 else pltpu.roll(halo_w, 128 - c, 1)
                            side = jnp.where(lane == 0, edge, pltpu.roll(old, 1, 1))
                        else:
                            c = f * HALF + WESTWARD.index(j)
                            edge = pltpu.roll(halo_e, 127 - c, 1)
                            side = jnp.where(lane == 127, edge, pltpu.roll(old, 127, 1))
                        r = f * HALF + (j if SIN[j] > 0 else j - HALF)
                        if SIN[j] > 0:
                            row = row_recv[slot, 0, k, pl.ds(r, 1), :]
                            above = jnp.where(sub == 0, row, pltpu.roll(old, 1, 0))
                        else:
                            row = row_recv[slot, 1, k, pl.ds(r, 1), :]
                            above = jnp.where(sub == 7, row, pltpu.roll(old, 7, 0))
                        new = mask * (rate_0 * old + rate_x * side + rate_y * above)
                        if part == 0:
                            state[step, f, k, PAD + j] = new
                            parts = pack_bin(slot + 1, f, k, j, new, parts)
                        else:
                            write_state(step, f, k, j, new)
                if part == 0:
                    return join(sums, parts, kk)
                return sums

            sums = lax.fori_loop(0, GROUP, at_level, (zeros, zeros))
            if part == 0:
                finish_pack(slot + 1, g, sums)
                send_halo(slot + 1, g)
            else:

                @pl.when(jnp.logical_and(g == 0, has_down))
                def _():
                    band_copy(step, 1).start()

                @pl.when(jnp.logical_and(g == groups - 1, has_up))
                def _():
                    band_copy(step, 0).start()

            return 0

        lax.fori_loop(0, groups, group, 0)

    def wrap(ext, first):
        def one(i, _):
            f, k = i // FH, first + lax.rem(i, FH)
            ext[f, k, pl.ds(0, PAD)] = ext[f, k, pl.ds(ND, PAD)]
            ext[f, k, pl.ds(ND + PAD, PAD)] = ext[f, k, pl.ds(PAD, PAD)]
            return 0

        lax.fori_loop(0, 2 * FH, one, 0)

    def lend(ext, step, first, k0):
        def one(i, _):
            f, k = i // (FH - 1), lax.rem(i, FH - 1)
            ext[f, first + k] = state[step, f, k0 + k]
            return 0

        lax.fori_loop(0, 2 * (FH - 1), one, 0)

    def source(step, g, upper, lower):
        up = jnp.maximum(freq_off[0], 1)
        down = jnp.maximum(freq_off[1], 1)
        e = dir_off[0]
        h = dir_off[1]
        slot = 2 * step + 2

        def at_level(kk, sums):
            k = g * GROUP + kk
            strength = source_step * coupling[k]
            parts = [zeros, zeros]
            for j in range(ND):
                f0 = state[step, 0, k, PAD + j]
                g0 = state[step, 1, k, PAD + j]
                fp1, gp1 = upper(k + up, j + e)
                fm1, gm1 = lower(k - down, j - h)
                fp2, gp2 = upper(k + up, j - e)
                fm2, gm2 = lower(k - down, j + h)
                linear = weight_plus * (fp1 + fp2) + weight_minus * (fm1 + fm2)
                linear_t = weight_plus * (gp1 + gp2) + weight_minus * (gm1 + gm2)
                cross = weight_cross * (fp1 * fm1 + fp2 * fm2)
                cross_t = weight_cross * (gp1 * fm1 + fp1 * gm1 + gp2 * fm2 + fp2 * gm2)
                lead = f0 * linear
                rest = lead - cross
                rate = f0 * rest
                change = g0 * (lead + rest) + f0 * (f0 * linear_t - cross_t)
                for f, new in ((0, f0 - strength * rate), (1, g0 - strength * change)):
                    if step < STEPS - 1:
                        state[step + 1, f, k, PAD + j] = new
                        parts = pack_bin(slot, f, k, j, new, parts)
                    else:
                        outputs[f][k, j, 0] = new
            return join(sums, parts, kk) if step < STEPS - 1 else sums

        sums = lax.fori_loop(0, GROUP, at_level, (zeros, zeros))
        if step < STEPS - 1:
            finish_pack(slot, g, sums)
            send_halo(slot, g)

    def model_step(step):
        low_ext, high_ext = low_exts[step], high_exts[step]
        substep(step, 0)
        substep(step, 1)

        def local(k, j):
            return state[step, 0, k, PAD + j], state[step, 1, k, PAD + j]

        def low(k, j):
            return low_ext[0, k + FH, PAD + j], low_ext[1, k + FH, PAD + j]

        def high(k, j):
            i = k - (n_k - FH + 1)
            return high_ext[0, i, PAD + j], high_ext[1, i, PAD + j]

        source(step, 1, local, local)
        lend(low_ext, step, FH, 0)
        lend(high_ext, step, 0, n_k - FH + 1)

        @pl.when(has_down)
        def _():
            band_copy(step, 0).wait_recv()
            wrap(low_ext, 0)

        source(step, 0, local, low)

        @pl.when(has_up)
        def _():
            band_copy(step, 1).wait_recv()
            wrap(high_ext, FH - 1)

        source(step, groups - 1, high, local)

    for step in range(STEPS):
        model_step(step)

    def drain(i, _):
        slot, g = i // groups, lax.rem(i, groups)

        @pl.when(has_north)
        def _():
            row_copy(slot, 0, g).wait_send()

        @pl.when(has_south)
        def _():
            row_copy(slot, 1, g).wait_send()

        col_copy(slot, 0, g).wait_send()
        col_copy(slot, 1, g).wait_send()
        return 0

    lax.fori_loop(0, 2 * STEPS * groups, drain, 0)
    for step in range(STEPS):

        @pl.when(has_up)
        def _():
            band_copy(step, 0).wait_send()

        @pl.when(has_down)
        def _():
            band_copy(step, 1).wait_send()


def body(background, tangent, sea_mask, coupling, freq_offsets, dir_offsets):
    n_k = background.shape[0]
    groups = n_k // GROUP
    slots = 2 * STEPS
    f32 = jnp.float32
    dma = pltpu.SemaphoreType.DMA
    out = jax.ShapeDtypeStruct(background.shape, f32)
    return pl.pallas_call(
        lambda *refs: kernel(n_k, *refs),
        out_shape=(out, out),
        in_specs=[
            pl.BlockSpec(memory_space=pltpu.VMEM),
            pl.BlockSpec(memory_space=pltpu.VMEM),
            pl.BlockSpec(memory_space=pltpu.VMEM),
            pl.BlockSpec(memory_space=pltpu.SMEM),
            pl.BlockSpec(memory_space=pltpu.SMEM),
            pl.BlockSpec(memory_space=pltpu.SMEM),
        ],
        out_specs=(pl.BlockSpec(memory_space=pltpu.VMEM), pl.BlockSpec(memory_space=pltpu.VMEM)),
        scratch_shapes=[
            pltpu.VMEM((STEPS, 2, n_k, WIDE, 8, 128), f32),
            pltpu.VMEM((2, 2 * FH - 1, WIDE, 8, 128), f32),
            pltpu.VMEM((2, 2 * FH - 1, WIDE, 8, 128), f32),
            pltpu.VMEM((2, 2 * FH - 1, WIDE, 8, 128), f32),
            pltpu.VMEM((2, 2 * FH - 1, WIDE, 8, 128), f32),
            pltpu.VMEM((slots, 2, n_k, ND, 128), f32),
            pltpu.VMEM((slots, 2, n_k, ND, 128), f32),
            pltpu.VMEM((slots, 2, groups, 8, 128), f32),
            pltpu.VMEM((slots, 2, groups, 8, 128), f32),
            pltpu.SMEM((n_k,), f32),
            dma((slots, 2, groups)),
            dma((slots, 2, groups)),
            dma((slots, 2, groups)),
            dma((slots, 2, groups)),
            dma((STEPS, 2)),
            dma((STEPS, 2)),
        ],
        compiler_params=pltpu.CompilerParams(
            collective_id=0, has_side_effects=True, vmem_limit_bytes=48 * 1024 * 1024
        ),
        name="wave_steps",
    )(background, tangent, sea_mask, coupling, freq_offsets, dir_offsets)


def solution(mesh):
    in_specs = (
        P("band", None, "tile", None, None),
        P("band", None, "tile", None, None),
        P("tile", None, None),
        P("band"),
        P(),
        P(),
    )
    out_specs = (P("band", None, "tile", None, None), P("band", None, "tile", None, None))
    return jax.shard_map(body, mesh=mesh, in_specs=in_specs, out_specs=out_specs, check_vma=False)
```

profile of v0, /device:TPU:1, one launch (start us, length us, event | category | flops | bytes accessed | tf_op | source)
XLA Modules:
  0.0 79.9 jit_solution(15538886940930491616)
XLA Ops:
  0.6 0.0 copy-start
  0.6 1.3 %copy-done = f32[9,36,1,8,128]{4,3,2,1,0:T(8,128)S(1)} copy-done((f32[9,36,1,8,128]{4,3,2,1,0:T(8,128)S(1)}, f32[9,36,1,8,128]{4,3,2,1,0:T(8,128)}, u32[]{:S(2)}) %copy-start) | copy-done | bytes 1327128
  2.0 0.0 copy-start.1
  2.0 1.3 %copy-done.1 = f32[9,36,1,8,128]{4,3,2,1,0:T(8,128)S(1)} copy-done((f32[9,36,1,8,128]{4,3,2,1,0:T(8,128)S(1)}, f32[9,36,1,8,128]{4,3,2,1,0:T(8,128)}, u32[]{:S(2)}) %copy-start.1) | copy-done | bytes 1327128
  3.3 0.0 copy-start.2
  3.3 0.7 copy-done.2
  4.0 0.0 copy-start.3
  4.0 0.7 copy-done.3
  4.6 0.0 copy-start.4
  4.6 0.7 copy-done.4
  5.3 0.0 copy-start.5
  5.3 0.7 copy-done.5
  5.9 71.9 %wave_steps.1 = (f32[9,36,1,8,128]{4,3,2,1,0:T(8,128)S(1)}, f32[9,36,1,8,128]{4,3,2,1,0:T(8,128)S(1)}) custom-call(f32[9,36,1,8,128]{4,3,2,1,0:T(8,128)S(1)} %copy-done, f32[9,36,1,8,128]{4,3,2,1,0:T(8,128)S(1)} %copy-done.1, s32[1,8,128]{2,1,0:T(8,128)S(1)} %copy-done.2, f32[9]{0:T(128)S(1)} %copy-done.3, s32[2]{0:T(128)S(1)} %copy-done.4, s32[2]{0:T(128)S(1)} %copy-done.5), custom_call_target="tpu_custom_call" | custom-call | tf_op jit(solution)/shard_map/wave_steps/pallas_call | solution.py:441
  77.8 1.1 %copy.10 = f32[9,36,1,8,128]{4,3,2,1,0:T(8,128)} copy(f32[9,36,1,8,128]{4,3,2,1,0:T(8,128)S(1)} %get-tuple-element.4) | data formatting | bytes 2654208
  78.9 1.1 %copy.11 = f32[9,36,1,8,128]{4,3,2,1,0:T(8,128)} copy(f32[9,36,1,8,128]{4,3,2,1,0:T(8,128)S(1)} %get-tuple-element.5) | data formatting | bytes 2654208
Async XLA Ops:
  0.6 1.3 %copy-start = (f32[9,36,1,8,128]{4,3,2,1,0:T(8,128)S(1)}, f32[9,36,1,8,128]{4,3,2,1,0:T(8,128)}, u32[]{:S(2)}) copy-start(f32[9,36,1,8,128]{4,3,2,1,0:T(8,128)} %refs_0_.1) | copy-start | bytes 3981316
  2.0 1.3 %copy-start.1 = (f32[9,36,1,8,128]{4,3,2,1,0:T(8,128)S(1)}, f32[9,36,1,8,128]{4,3,2,1,0:T(8,128)}, u32[]{:S(2)}) copy-start(f32[9,36,1,8,128]{4,3,2,1,0:T(8,128)} %refs_1_.1) | copy-start | bytes 3981316
  3.3 0.7 copy-start.2
  4.0 0.7 copy-start.3
  4.6 0.7 copy-start.4
  5.3 0.7 copy-start.5
where the time goes:
time: 80.2 us; the launch traced here: 79.9 us
  Pallas kernels  71.9 us (90%)
  local copies, waits for them, and re-layouts  7.41 us (9%)
    pallas_call x1, Pallas kernels, body(): pl.pallas_call(lambda *refs: kernel(n_k, *refs), out_shape=(out, out), in...  71.9 us
    unnamed x14, local copies, waits for them, and re-layouts  7.41 us

commit v1 on v0

--- a/solution.py
+++ b/solution.py
@@ -34,13 +34,14 @@
     n_k,
     back_in,
     tang_in,
-    mask_in,
-    coupling,
-    freq_off,
-    dir_off,
+    mask_hbm,
+    coupling_hbm,
+    freq_hbm,
+    dir_hbm,
     back_out,
     tang_out,
-    state,
+    state_0,
+    state_1,
     low_ext_0,
     low_ext_1,
     high_ext_0,
@@ -49,7 +50,15 @@
     row_recv,
     col_send,
     col_recv,
+    mask_in,
+    coupling,
+    freq_off,
+    dir_off,
     speed,
+    result,
+    load_sem,
+    store_sem,
+    small_sem,
     row_ssem,
     row_rsem,
     col_ssem,
@@ -71,10 +80,37 @@
     has_up = band < bands - 1
     has_down = band > 0
     groups = n_k // GROUP
+    states = (state_0, state_1)
     low_exts = (low_ext_0, low_ext_1)
     high_exts = (high_ext_0, high_ext_1)
     inputs = (back_in, tang_in)
     outputs = (back_out, tang_out)
+
+    def load_copy(f, g):
+        return pltpu.make_async_copy(
+            inputs[f].at[pl.ds(g * GROUP, GROUP), :, 0],
+            state_0.at[f, pl.ds(g * GROUP, GROUP), pl.ds(PAD, ND)],
+            load_sem.at[f, g],
+        )
+
+    def store_copy(f, g):
+        return pltpu.make_async_copy(
+            result.at[f, pl.ds(g * GROUP, GROUP)],
+            outputs[f].at[pl.ds(g * GROUP, GROUP), :, 0],
+            store_sem.at[f, g],
+        )
+
+    small = [
+        pltpu.make_async_copy(src, dst, small_sem.at[i])
+        for i, (src, dst) in enumerate(
+            (
+                (mask_hbm, mask_in),
+                (coupling_hbm, coupling),
+                (freq_hbm, freq_off),
+                (dir_hbm, dir_off),
+            )
+        )
+    ]
 
     def row_copy(slot, side, g):
         ks = pl.ds(g * GROUP, GROUP)
@@ -99,11 +135,11 @@
 
     def band_copy(step, side):
         if side == 0:
-            src = state.at[step, :, pl.ds(n_k - FH, FH), pl.ds(PAD, ND)]
+            src = states[step].at[:, pl.ds(n_k - FH, FH), pl.ds(PAD, ND)]
             dst = low_exts[step].at[:, pl.ds(0, FH), pl.ds(PAD, ND)]
             target = lax.rem(band + 1, bands)
         else:
-            src = state.at[step, :, pl.ds(0, FH), pl.ds(PAD, ND)]
+            src = states[step].at[:, pl.ds(0, FH), pl.ds(PAD, ND)]
             dst = high_exts[step].at[:, pl.ds(FH - 1, FH), pl.ds(PAD, ND)]
             target = lax.rem(band + bands - 1, bands)
         return pltpu.make_async_remote_copy(
@@ -139,6 +175,12 @@
         col_copy(slot, 0, g).wait_recv()
         col_copy(slot, 1, g).wait_recv()
 
+    for copy in small:
+        copy.start()
+    for g in (0, 2, 1):
+        for f in range(2):
+            load_copy(f, g).start()
+
     barrier = pltpu.get_barrier_semaphore()
     for cond, target in (
         (None, {"tile": east}),
@@ -165,12 +207,14 @@
 
     lane = lax.broadcasted_iota(jnp.int32, (8, 128), 1)
     sub = lax.broadcasted_iota(jnp.int32, (8, 128), 0)
+    for copy in small:
+        copy.wait()
     mask = mask_in[0].astype(jnp.float32)
     zeros = jnp.zeros((8, 128), jnp.float32)
 
     def zero_rows(side):
         def slots(i, _):
-            row_recv[i // n_k, side, lax.rem(i, n_k)] = jnp.zeros((ND, 128), jnp.float32)
+            row_recv[i // n_k, side, lax.rem(i, n_k)] = jnp.zeros((2, HALF, 128), jnp.float32)
             return 0
 
         lax.fori_loop(0, 2 * STEPS * n_k, slots, 0)
@@ -189,48 +233,47 @@
         pl.when(jnp.logical_not(has_down))(lambda: zero_ext(low_exts[step], 0))
         pl.when(jnp.logical_not(has_up))(lambda: zero_ext(high_exts[step], FH - 1))
 
-    def pack_bin(slot, f, k, j, new, parts):
-        r = f * HALF + (j if SIN[j] > 0 else j - HALF)
-        if SIN[j] > 0:
-            row_send[slot, 0, k, pl.ds(r, 1), :] = new[7:8, :]
-        else:
-            row_send[slot, 1, k, pl.ds(r, 1), :] = new[0:1, :]
+    def pack_bin(f, kk, j, new, parts):
         if COS[j] > 0:
-            c = f * HALF + EASTWARD.index(j)
+            c = kk * ND + f * HALF + EASTWARD.index(j)
             moved = pltpu.roll(new, (c + 1) % 128, 1)
             return [jnp.where(lane == c, moved, parts[0]), parts[1]]
-        c = f * HALF + WESTWARD.index(j)
+        c = kk * ND + f * HALF + WESTWARD.index(j)
         moved = new if c == 0 else pltpu.roll(new, c, 1)
         return [parts[0], jnp.where(lane == c, moved, parts[1])]
 
-    def join(sums, parts, i):
-        return tuple(s + pltpu.roll(p, i * ND, 1) for s, p in zip(sums, parts))
-
-    def finish_pack(slot, g, sums):
-        col_send[slot, 0, g] = sums[0]
-        col_send[slot, 1, g] = sums[1]
+    def finish_pack(state, slot, g, parts):
+        rows = state.reshape(2, n_k, WIDE * 8, 128)
+        for kk in range(GROUP):
+            k = g * GROUP + kk
+            for f in range(2):
+                row_send[slot, 0, k, f] = rows[f, k, pl.ds(8 * PAD + 7, HALF, stride=8), :]
+                row_send[slot, 1, k, f] = rows[f, k, pl.ds(8 * (PAD + HALF), HALF, stride=8), :]
+        col_send[slot, 0, g] = parts[0]
+        col_send[slot, 1, g] = parts[1]
 
     def write_state(step, f, k, j, new):
-        state[step, f, k, PAD + j] = new
+        state = states[step]
+        state[f, k, PAD + j] = new
         if j >= ND - PAD:
-            state[step, f, k, j - (ND - PAD)] = new
+            state[f, k, j - (ND - PAD)] = new
         if j < PAD:
-            state[step, f, k, PAD + ND + j] = new
+            state[f, k, PAD + ND + j] = new
 
     def entry(i, _):
         g = lax.rem(2 * i, groups)
 
-        def at_level(kk, sums):
+        for f in range(2):
+            load_copy(f, g).wait()
+        parts = [zeros, zeros]
+        for kk in range(GROUP):
             k = g * GROUP + kk
-            parts = [zeros, zeros]
             for f in range(2):
                 for j in range(ND):
-                    new = inputs[f][k, j, 0] * mask
-                    state[0, f, k, PAD + j] = new
-                    parts = pack_bin(0, f, k, j, new, parts)
-            return join(sums, parts, kk)
-
-        finish_pack(0, g, lax.fori_loop(0, GROUP, at_level, (zeros, zeros)))
+                    new = state_0[f, k, PAD + j] * mask
+                    state_0[f, k, PAD + j] = new
+                    parts = pack_bin(f, kk, j, new, parts)
+        finish_pack(state_0, 0, g, parts)
         return 0
 
     lax.fori_loop(0, groups, entry, 0)
@@ -256,47 +299,47 @@
             col_low = col_recv[slot, 0, g]
             col_high = col_recv[slot, 1, g]
 
-            def at_level(kk, sums):
+            for kk in range(GROUP):
                 k = g * GROUP + kk
                 rate = speed[k]
-                back = lax.rem(128 - kk * ND, 128)
-                halo_w = pltpu.roll(col_low, back, 1)
-                halo_e = pltpu.roll(col_high, back, 1)
-                parts = [zeros, zeros]
                 for j in range(ND):
                     rate_x = rate * jnp.float32(abs(COS[j]))
                     rate_y = rate * jnp.float32(abs(SIN[j]))
                     rate_0 = jnp.float32(1.0) - rate_x - rate_y
                     for f in range(2):
-                        old = state[step, f, k, PAD + j]
+                        old = states[step][f, k, PAD + j]
                         if COS[j] > 0:
-                            c = f * HALF + EASTWARD.index(j)
-                            edge = halo_w if c == 0 else pltpu.roll(halo_w, 128 - c, 1)
+                            c = kk * ND + f * HALF + EASTWARD.index(j)
+                            edge = col_low if c == 0 else pltpu.roll(col_low, 128 - c, 1)
                             side = jnp.where(lane == 0, edge, pltpu.roll(old, 1, 1))
                         else:
-                            c = f * HALF + WESTWARD.index(j)
-                            edge = pltpu.roll(halo_e, 127 - c, 1)
+                            c = kk * ND + f * HALF + WESTWARD.index(j)
+                            edge = pltpu.roll(col_high, 127 - c, 1)
                             side = jnp.where(lane == 127, edge, pltpu.roll(old, 127, 1))
-                        r = f * HALF + (j if SIN[j] > 0 else j - HALF)
+                        r = j if SIN[j] > 0 else j - HALF
                         if SIN[j] > 0:
-                            row = row_recv[slot, 0, k, pl.ds(r, 1), :]
+                            row = row_recv[slot, 0, k, f, pl.ds(r, 1), :]
                             above = jnp.where(sub == 0, row, pltpu.roll(old, 1, 0))
                         else:
-                            row = row_recv[slot, 1, k, pl.ds(r, 1), :]
+                            row = row_recv[slot, 1, k, f, pl.ds(r, 1), :]
                             above = jnp.where(sub == 7, row, pltpu.roll(old, 7, 0))
                         new = mask * (rate_0 * old + rate_x * side + rate_y * above)
                         if part == 0:
-                            state[step, f, k, PAD + j] = new
-                            parts = pack_bin(slot + 1, f, k, j, new, parts)
+                            states[step][f, k, PAD + j] = new
                         else:
                             write_state(step, f, k, j, new)
-                if part == 0:
-                    return join(sums, parts, kk)
-                return sums
-
-            sums = lax.fori_loop(0, GROUP, at_level, (zeros, zeros))
             if part == 0:
-                finish_pack(slot + 1, g, sums)
+
+                @pl.when(g >= 0)
+                def _():
+                    parts = [zeros, zeros]
+                    for kk in range(GROUP):
+                        k = g * GROUP + kk
+                        for f in range(2):
+                            for j in range(ND):
+                                parts = pack_bin(f, kk, j, states[step][f, k, PAD + j], parts)
+                    finish_pack(states[step], slot + 1, g, parts)
+
                 send_halo(slot + 1, g)
             else:
 
@@ -324,7 +367,7 @@
     def lend(ext, step, first, k0):
         def one(i, _):
             f, k = i // (FH - 1), lax.rem(i, FH - 1)
-            ext[f, first + k] = state[step, f, k0 + k]
+            ext[f, first + k] = states[step][f, k0 + k]
             return 0
 
         lax.fori_loop(0, 2 * (FH - 1), one, 0)
@@ -336,13 +379,13 @@
         h = dir_off[1]
         slot = 2 * step + 2
 
-        def at_level(kk, sums):
+        parts = [zeros, zeros]
+        for kk in range(GROUP):
             k = g * GROUP + kk
             strength = source_step * coupling[k]
-            parts = [zeros, zeros]
             for j in range(ND):
-                f0 = state[step, 0, k, PAD + j]
-                g0 = state[step, 1, k, PAD + j]
+                f0 = states[step][0, k, PAD + j]
+                g0 = states[step][1, k, PAD + j]
                 fp1, gp1 = upper(k + up, j + e)
                 fm1, gm1 = lower(k - down, j - h)
                 fp2, gp2 = upper(k + up, j - e)
@@ -357,16 +400,16 @@
                 change = g0 * (lead + rest) + f0 * (f0 * linear_t - cross_t)
                 for f, new in ((0, f0 - strength * rate), (1, g0 - strength * change)):
                     if step < STEPS - 1:
-                        state[step + 1, f, k, PAD + j] = new
-                        parts = pack_bin(slot, f, k, j, new, parts)
+                        states[step + 1][f, k, PAD + j] = new
+                        parts = pack_bin(f, kk, j, new, parts)
                     else:
-                        outputs[f][k, j, 0] = new
-            return join(sums, parts, kk) if step < STEPS - 1 else sums
-
-        sums = lax.fori_loop(0, GROUP, at_level, (zeros, zeros))
+                        result[f, k, j] = new
         if step < STEPS - 1:
-            finish_pack(slot, g, sums)
+            finish_pack(states[step + 1], slot, g, parts)
             send_halo(slot, g)
+        else:
+            for f in range(2):
+                store_copy(f, g).start()
 
     def model_step(step):
         low_ext, high_ext = low_exts[step], high_exts[step]
@@ -374,7 +417,7 @@
         substep(step, 1)
 
         def local(k, j):
-            return state[step, 0, k, PAD + j], state[step, 1, k, PAD + j]
+            return states[step][0, k, PAD + j], states[step][1, k, PAD + j]
 
         def low(k, j):
             return low_ext[0, k + FH, PAD + j], low_ext[1, k + FH, PAD + j]
@@ -403,6 +446,10 @@
 
     for step in range(STEPS):
         model_step(step)
+
+    for g in range(groups):
+        for f in range(2):
+            store_copy(f, g).wait()
 
     def drain(i, _):
         slot, g = i // groups, lax.rem(i, groups)
@@ -441,26 +488,28 @@
     return pl.pallas_call(
         lambda *refs: kernel(n_k, *refs),
         out_shape=(out, out),
-        in_specs=[
-            pl.BlockSpec(memory_space=pltpu.VMEM),
-            pl.BlockSpec(memory_space=pltpu.VMEM),
-            pl.BlockSpec(memory_space=pltpu.VMEM),
-            pl.BlockSpec(memory_space=pltpu.SMEM),
-            pl.BlockSpec(memory_space=pltpu.SMEM),
-            pl.BlockSpec(memory_space=pltpu.SMEM),
-        ],
-        out_specs=(pl.BlockSpec(memory_space=pltpu.VMEM), pl.BlockSpec(memory_space=pltpu.VMEM)),
+        in_specs=[pl.BlockSpec(memory_space=pltpu.HBM)] * 6,
+        out_specs=(pl.BlockSpec(memory_space=pl.ANY), pl.BlockSpec(memory_space=pl.ANY)),
         scratch_shapes=[
-            pltpu.VMEM((STEPS, 2, n_k, WIDE, 8, 128), f32),
+            pltpu.VMEM((2, n_k, WIDE, 8, 128), f32),
+            pltpu.VMEM((2, n_k, WIDE, 8, 128), f32),
             pltpu.VMEM((2, 2 * FH - 1, WIDE, 8, 128), f32),
             pltpu.VMEM((2, 2 * FH - 1, WIDE, 8, 128), f32),
             pltpu.VMEM((2, 2 * FH - 1, WIDE, 8, 128), f32),
             pltpu.VMEM((2, 2 * FH - 1, WIDE, 8, 128), f32),
-            pltpu.VMEM((slots, 2, n_k, ND, 128), f32),
-            pltpu.VMEM((slots, 2, n_k, ND, 128), f32),
+            pltpu.VMEM((slots, 2, n_k, 2, HALF, 128), f32),
+            pltpu.VMEM((slots, 2, n_k, 2, HALF, 128), f32),
             pltpu.VMEM((slots, 2, groups, 8, 128), f32),
             pltpu.VMEM((slots, 2, groups, 8, 128), f32),
+            pltpu.VMEM((1, 8, 128), jnp.int32),
             pltpu.SMEM((n_k,), f32),
+            pltpu.SMEM((2,), jnp.int32),
+            pltpu.SMEM((2,), jnp.int32),
+            pltpu.SMEM((n_k,), f32),
+            pltpu.VMEM((2, n_k, ND, 8, 128), f32),
+            dma((2, groups)),
+            dma((2, groups)),
+            dma((4,)),
             dma((slots, 2, groups)),
             dma((slots, 2, groups)),
             dma((slots, 2, groups)),
@@ -469,7 +518,7 @@
             dma((STEPS, 2)),
         ],
         compiler_params=pltpu.CompilerParams(
-            collective_id=0, has_side_effects=True, vmem_limit_bytes=48 * 1024 * 1024
+            collective_id=0, has_side_effects=True, vmem_limit_bytes=67043328
         ),
         name="wave_steps",
     )(background, tangent, sea_mask, coupling, freq_offsets, dir_offsets)

time: 80.2 us -> 74.5 us (0.929)
  local copies, waits for them, and re-layouts: 7.41 us -> 3.64 us
  Pallas kernels: 71.9 us -> 70.1 us
    unnamed x14 -> x4, local copies, waits for them, and re-layouts: 7.41 us -> 3.64 us
    pallas_call x1, Pallas kernels: 71.9 us -> 70.1 us  [body(): pl.pallas_call(lambda *refs: kernel(n_k, *refs), out_shape=(out, out), in...]
where the time goes in v1:
time: 74.5 us; the launch traced here: 74.4 us
  Pallas kernels  70.1 us (94%)
  local copies, waits for them, and re-layouts  3.64 us (5%)
    pallas_call x1, Pallas kernels, body(): pl.pallas_call(lambda *refs: kernel(n_k, *refs), out_shape=(out, out), in...  70.1 us
    unnamed x4, local copies, waits for them, and re-layouts  3.64 us

profile of v1, /device:TPU:1, one launch (start us, length us, event | category | flops | bytes accessed | tf_op | source)
XLA Modules:
  0.0 74.4 jit_solution(6843044182114399636)
XLA Ops:
  0.6 70.1 %wave_steps.1 = (f32[9,36,1,8,128]{4,3,2,1,0:T(8,128)}, f32[9,36,1,8,128]{4,3,2,1,0:T(8,128)}) custom-call(f32[9,36,1,8,128]{4,3,2,1,0:T(8,128)} %refs_0_.1, f32[9,36,1,8,128]{4,3,2,1,0:T(8,128)} %refs_1_.1, s32[1,8,128]{2,1,0:T(8,128)} %refs_2_.1, f32[9]{0:T(128)} %refs_3_.1, s32[2]{0:T(128)} %refs_4_.1, s32[2]{0:T(128)} %refs_5_.1), custom_call_target="tpu_custom_call" | custom-call | tf_op jit(solution)/shard_map/wave_steps/pallas_call | solution.py:488
  70.7 0.0 copy-start
  70.7 2.6 %copy.10 = f32[9,36,1,8,128]{4,3,2,1,0:T(8,128)} copy(f32[9,36,1,8,128]{4,3,2,1,0:T(8,128)} %get-tuple-element.4) | data formatting | bytes 2654208
  73.3 0.0 copy-done
  73.3 1.1 %copy.11 = f32[9,36,1,8,128]{4,3,2,1,0:T(8,128)} copy(f32[9,36,1,8,128]{4,3,2,1,0:T(8,128)S(1)} %copy-done) | data formatting | bytes 2654208
Async XLA Ops:
  70.7 2.6 %copy-start = (f32[9,36,1,8,128]{4,3,2,1,0:T(8,128)S(1)}, f32[9,36,1,8,128]{4,3,2,1,0:T(8,128)}, u32[]{:S(2)}) copy-start(f32[9,36,1,8,128]{4,3,2,1,0:T(8,128)} %get-tuple-element.5) | copy-start | bytes 3981316

commit v2 on v1

--- a/solution.py
+++ b/solution.py
@@ -55,9 +55,7 @@
     freq_off,
     dir_off,
     speed,
-    result,
     load_sem,
-    store_sem,
     small_sem,
     row_ssem,
     row_rsem,
@@ -91,13 +89,6 @@
             inputs[f].at[pl.ds(g * GROUP, GROUP), :, 0],
             state_0.at[f, pl.ds(g * GROUP, GROUP), pl.ds(PAD, ND)],
             load_sem.at[f, g],
-        )
-
-    def store_copy(f, g):
-        return pltpu.make_async_copy(
-            result.at[f, pl.ds(g * GROUP, GROUP)],
-            outputs[f].at[pl.ds(g * GROUP, GROUP), :, 0],
-            store_sem.at[f, g],
         )
 
     small = [
@@ -403,13 +394,10 @@
                         states[step + 1][f, k, PAD + j] = new
                         parts = pack_bin(f, kk, j, new, parts)
                     else:
-                        result[f, k, j] = new
+                        outputs[f][k, j, 0] = new
         if step < STEPS - 1:
             finish_pack(states[step + 1], slot, g, parts)
             send_halo(slot, g)
-        else:
-            for f in range(2):
-                store_copy(f, g).start()
 
     def model_step(step):
         low_ext, high_ext = low_exts[step], high_exts[step]
@@ -446,10 +434,6 @@
 
     for step in range(STEPS):
         model_step(step)
-
-    for g in range(groups):
-        for f in range(2):
-            store_copy(f, g).wait()
 
     def drain(i, _):
         slot, g = i // groups, lax.rem(i, groups)
@@ -489,7 +473,7 @@
         lambda *refs: kernel(n_k, *refs),
         out_shape=(out, out),
         in_specs=[pl.BlockSpec(memory_space=pltpu.HBM)] * 6,
-        out_specs=(pl.BlockSpec(memory_space=pl.ANY), pl.BlockSpec(memory_space=pl.ANY)),
+        out_specs=(pl.BlockSpec(memory_space=pltpu.VMEM), pl.BlockSpec(memory_space=pltpu.VMEM)),
         scratch_shapes=[
             pltpu.VMEM((2, n_k, WIDE, 8, 128), f32),
             pltpu.VMEM((2, n_k, WIDE, 8, 128), f32),
@@ -506,8 +490,6 @@
             pltpu.SMEM((2,), jnp.int32),
             pltpu.SMEM((2,), jnp.int32),
             pltpu.SMEM((n_k,), f32),
-            pltpu.VMEM((2, n_k, ND, 8, 128), f32),
-            dma((2, groups)),
             dma((2, groups)),
             dma((4,)),
             dma((slots, 2, groups)),
@@ -518,10 +500,10 @@
             dma((STEPS, 2)),
         ],
         compiler_params=pltpu.CompilerParams(
-            collective_id=0, has_side_effects=True, vmem_limit_bytes=67043328
+            collective_id=0, has_side_effects=True, vmem_limit_bytes=48 * 1024 * 1024
         ),
         name="wave_steps",
-    )(background, tangent, sea_mask, coupling, freq_offsets, dir_offsets)
+    )(*[pltpu.with_memory_space_constraint(x, pltpu.HBM) for x in (background, tangent, sea_mask, coupling, freq_offsets, dir_offsets)])
 
 
 def solution(mesh):

time: 74.5 us -> 72 us (0.966)
  local copies, waits for them, and re-layouts: 3.64 us -> 2.13 us
  Pallas kernels: 70.1 us -> 69.1 us
    unnamed x4 -> x2, local copies, waits for them, and re-layouts: 3.64 us -> 2.13 us
    pallas_call x1, Pallas kernels: 70.1 us -> 69.1 us  [body(): pl.pallas_call(lambda *refs: kernel(n_k, *refs), out_shape=(out, out), in...]
where the time goes in v2:
time: 72 us; the launch traced here: 71.9 us
  Pallas kernels  69.1 us (96%)
  local copies, waits for them, and re-layouts  2.13 us (3%)
    pallas_call x1, Pallas kernels, body(): pl.pallas_call(lambda *refs: kernel(n_k, *refs), out_shape=(out, out), in...  69.1 us
    unnamed x2, local copies, waits for them, and re-layouts  2.13 us

profile of v2, /device:TPU:1, one launch (start us, length us, event | category | flops | bytes accessed | tf_op | source)
XLA Modules:
  0.0 71.9 jit_solution(686129627104614417)
XLA Ops:
  0.6 69.1 %wave_steps.1 = (f32[9,36,1,8,128]{4,3,2,1,0:T(8,128)S(1)}, f32[9,36,1,8,128]{4,3,2,1,0:T(8,128)S(1)}) custom-call(f32[9,36,1,8,128]{4,3,2,1,0:T(8,128)} %refs_0_.1, f32[9,36,1,8,128]{4,3,2,1,0:T(8,128)} %refs_1_.1, s32[1,8,128]{2,1,0:T(8,128)} %refs_2_.1, f32[9]{0:T(128)} %refs_3_.1, s32[2]{0:T(128)} %refs_4_.1, s32[2]{0:T(128)} %refs_5_.1), custom_call_target="tpu_custom_call" | custom-call | tf_op jit(solution)/shard_map/wave_steps/pallas_call | solution.py:472
  69.8 1.1 %copy.10 = f32[9,36,1,8,128]{4,3,2,1,0:T(8,128)} copy(f32[9,36,1,8,128]{4,3,2,1,0:T(8,128)S(1)} %get-tuple-element.4) | data formatting | bytes 2654208
  70.8 1.1 %copy.11 = f32[9,36,1,8,128]{4,3,2,1,0:T(8,128)} copy(f32[9,36,1,8,128]{4,3,2,1,0:T(8,128)S(1)} %get-tuple-element.5) | data formatting | bytes 2654208

commit v3 on v2

--- a/solution.py
+++ b/solution.py
@@ -78,6 +78,15 @@
     has_up = band < bands - 1
     has_down = band > 0
     groups = n_k // GROUP
+    first = jnp.where(band < bands // 2, groups - 1, 0)
+    second = groups - 1 - first
+
+    def urgent(i):
+        return jnp.where(i == 0, first, jnp.where(i == 1, second, 1))
+
+    def arrival(i):
+        return jnp.where(i == 0, 1, jnp.where(i == 1, second, first))
+
     states = (state_0, state_1)
     low_exts = (low_ext_0, low_ext_1)
     high_exts = (high_ext_0, high_ext_1)
@@ -252,7 +261,7 @@
             state[f, k, PAD + ND + j] = new
 
     def entry(i, _):
-        g = lax.rem(2 * i, groups)
+        g = urgent(i)
 
         for f in range(2):
             load_copy(f, g).wait()
@@ -278,14 +287,14 @@
     )
     pl.semaphore_wait(barrier, peers)
 
-    for g in (0, 2, 1):
-        send_halo(0, g)
+    for i in range(groups):
+        send_halo(0, urgent(i))
 
     def substep(step, part):
         slot = 2 * step + part
 
         def group(i, _):
-            g = lax.rem(2 * i + step, groups)
+            g = arrival(i) if slot == 2 else urgent(i)
             wait_halo(slot, g)
             col_low = col_recv[slot, 0, g]
             col_high = col_recv[slot, 1, g]
@@ -418,19 +427,32 @@
         lend(low_ext, step, FH, 0)
         lend(high_ext, step, 0, n_k - FH + 1)
 
-        @pl.when(has_down)
-        def _():
-            band_copy(step, 0).wait_recv()
-            wrap(low_ext, 0)
-
-        source(step, 0, local, low)
-
-        @pl.when(has_up)
-        def _():
-            band_copy(step, 1).wait_recv()
-            wrap(high_ext, FH - 1)
-
-        source(step, groups - 1, high, local)
+        def edge(i, _):
+            is_low = jnp.where(i == 0, second, first) == 0
+
+            @pl.when(jnp.logical_and(is_low, has_down))
+            def _():
+                band_copy(step, 0).wait_recv()
+                wrap(low_ext, 0)
+
+            @pl.when(is_low)
+            def _():
+                source(step, 0, local, low)
+
+            is_high = jnp.logical_not(is_low)
+
+            @pl.when(jnp.logical_and(is_high, has_up))
+            def _():
+                band_copy(step, 1).wait_recv()
+                wrap(high_ext, FH - 1)
+
+            @pl.when(is_high)
+            def _():
+                source(step, groups - 1, high, local)
+
+            return 0
+
+        lax.fori_loop(0, 2, edge, 0)
 
     for step in range(STEPS):
         model_step(step)

time: 72 us -> 71.4 us (level)
  no operation moved by 1% of the time
where the time goes in v3:
time: 71.4 us; the launch traced here: 71.3 us
  Pallas kernels  68.6 us (96%)
  local copies, waits for them, and re-layouts  2.13 us (3%)
    pallas_call x1, Pallas kernels, body(): pl.pallas_call(lambda *refs: kernel(n_k, *refs), out_shape=(out, out), in...  68.6 us
    unnamed x2, local copies, waits for them, and re-layouts  2.13 us

profile of v3, /device:TPU:1, one launch (start us, length us, event | category | flops | bytes accessed | tf_op | source)
XLA Modules:
  0.0 71.3 jit_solution(4330184958641949380)
XLA Ops:
  0.6 68.6 %wave_steps.1 = (f32[9,36,1,8,128]{4,3,2,1,0:T(8,128)S(1)}, f32[9,36,1,8,128]{4,3,2,1,0:T(8,128)S(1)}) custom-call(f32[9,36,1,8,128]{4,3,2,1,0:T(8,128)} %refs_0_.1, f32[9,36,1,8,128]{4,3,2,1,0:T(8,128)} %refs_1_.1, s32[1,8,128]{2,1,0:T(8,128)} %refs_2_.1, f32[9]{0:T(128)} %refs_3_.1, s32[2]{0:T(128)} %refs_4_.1, s32[2]{0:T(128)} %refs_5_.1), custom_call_target="tpu_custom_call" | custom-call | tf_op jit(solution)/shard_map/wave_steps/pallas_call | solution.py:494
  69.2 1.1 %copy.10 = f32[9,36,1,8,128]{4,3,2,1,0:T(8,128)} copy(f32[9,36,1,8,128]{4,3,2,1,0:T(8,128)S(1)} %get-tuple-element.4) | data formatting | bytes 2654208
  70.3 1.1 %copy.11 = f32[9,36,1,8,128]{4,3,2,1,0:T(8,128)} copy(f32[9,36,1,8,128]{4,3,2,1,0:T(8,128)S(1)} %get-tuple-element.5) | data formatting | bytes 2654208

commit v4 on v3

--- a/solution.py
+++ b/solution.py
@@ -85,7 +85,7 @@
         return jnp.where(i == 0, first, jnp.where(i == 1, second, 1))
 
     def arrival(i):
-        return jnp.where(i == 0, 1, jnp.where(i == 1, second, first))
+        return jnp.where(i == 0, second, jnp.where(i == 1, first, 1))
 
     states = (state_0, state_1)
     low_exts = (low_ext_0, low_ext_1)
@@ -406,7 +406,8 @@
                         outputs[f][k, j, 0] = new
         if step < STEPS - 1:
             finish_pack(states[step + 1], slot, g, parts)
-            send_halo(slot, g)
+            if g != 1:
+                send_halo(slot, g)
 
     def model_step(step):
         low_ext, high_ext = low_exts[step], high_exts[step]
@@ -453,6 +454,8 @@
             return 0
 
         lax.fori_loop(0, 2, edge, 0)
+        if step < STEPS - 1:
+            send_halo(2 * step + 2, 1)
 
     for step in range(STEPS):
         model_step(step)

time: 71.4 us -> 70.6 us (0.989)
  Pallas kernels: 68.6 us -> 67.7 us
    pallas_call x1, Pallas kernels: 68.6 us -> 67.7 us  [body(): pl.pallas_call(lambda *refs: kernel(n_k, *refs), out_shape=(out, out), in...]
where the time goes in v4:
time: 70.6 us; the launch traced here: 70.5 us
  Pallas kernels  67.7 us (96%)
  local copies, waits for them, and re-layouts  2.13 us (3%)
    pallas_call x1, Pallas kernels, body(): pl.pallas_call(lambda *refs: kernel(n_k, *refs), out_shape=(out, out), in...  67.7 us
    unnamed x2, local copies, waits for them, and re-layouts  2.13 us

profile of v4, /device:TPU:1, one launch (start us, length us, event | category | flops | bytes accessed | tf_op | source)
XLA Modules:
  0.0 70.5 jit_solution(4732948245965929623)
XLA Ops:
  0.6 67.7 %wave_steps.1 = (f32[9,36,1,8,128]{4,3,2,1,0:T(8,128)S(1)}, f32[9,36,1,8,128]{4,3,2,1,0:T(8,128)S(1)}) custom-call(f32[9,36,1,8,128]{4,3,2,1,0:T(8,128)} %refs_0_.1, f32[9,36,1,8,128]{4,3,2,1,0:T(8,128)} %refs_1_.1, s32[1,8,128]{2,1,0:T(8,128)} %refs_2_.1, f32[9]{0:T(128)} %refs_3_.1, s32[2]{0:T(128)} %refs_4_.1, s32[2]{0:T(128)} %refs_5_.1), custom_call_target="tpu_custom_call" | custom-call | tf_op jit(solution)/shard_map/wave_steps/pallas_call | solution.py:497
  68.4 1.1 %copy.10 = f32[9,36,1,8,128]{4,3,2,1,0:T(8,128)} copy(f32[9,36,1,8,128]{4,3,2,1,0:T(8,128)S(1)} %get-tuple-element.4) | data formatting | bytes 2654208
  69.4 1.1 %copy.11 = f32[9,36,1,8,128]{4,3,2,1,0:T(8,128)} copy(f32[9,36,1,8,128]{4,3,2,1,0:T(8,128)S(1)} %get-tuple-element.5) | data formatting | bytes 2654208
